TPU v7x, 256 devices: a whole 4x4x8 slice. The times are simulated.
256 devices in a mesh: seq: 64 (over x_hi, z, y), kvh: 4 (over x_lo, core).
Axes of the slice: x: 4 (x_hi: 2, x_lo: 2; x = x_hi * 2 + x_lo), y: 4, z: 8, core: 2. Of those that a mesh axis runs over, the one named last changes fastest.
Arguments:
- queries: bfloat16 [8192, 8192], P('seq', 'kvh'), may hold values from -100 to 100
- keys: bfloat16 [8192, 1024], P('seq', 'kvh'), may hold values from -4 to 4
- values: bfloat16 [8192, 1024], P('seq', 'kvh'), may hold values from -6 to 6
- segments: int32 [8192], P('seq'), may hold values from 0 to 2, never falling along the last dimension, each value on 1 to 4224 neighbouring positions
- basis: bfloat16 [8, 2, 128, 32], P('kvh'), may hold values from -0.5 to 0.5
Outputs:
- attention: bfloat16 [8192, 8192], P('seq', 'kvh')
- latents: bfloat16 [8192, 512], P('seq', 'kvh')
- captured: float32 [8, 2, 32, 32], P('kvh')
- share: float32 [8, 2], P('kvh')
Inputs may be any that keep to these rules, and one draw needn't show every extreme that they name: `segments`: document ids never fall along the sequence, and each document has at most 4224 tokens.
All inputs are finite; a program needn't handle non-finite values.
Results may differ from a plain program's by a relative error of at most 0.004.
Values may be sent and summed in bfloat16 or wider, within the bound.
No kernel may reach another device: no remote copies, remote signals or barrier semaphores. Data moves between devices by JAX's collectives and lax.ppermute only.
A program may use at most 64 MiB of HBM per device.

v0:
```python
import math

import jax
import jax.numpy as jnp
from jax import lax
from jax.sharding import Mesh
from jax.sharding import PartitionSpec as P

HD = 128
QH = 64
KVH = 8
RANK = 32
SEQ = ("seq_0", "seq_1", "seq_2")


def sent_together(arrays, axis, dim, along):
    widths = [math.prod(a.shape[along:]) for a in arrays]
    both = jnp.concatenate(
        [a.reshape(*a.shape[:along], w) for a, w in zip(arrays, widths)], axis=along
    )
    result = lax.all_gather(both, axis, axis=dim, tiled=True)
    blocks = jnp.split(result, [sum(widths[:k]) for k in range(1, len(widths))], axis=along)
    return tuple(
        (b.reshape(*result.shape[:along], *a.shape[along:]) for a, b in zip(arrays, blocks))
    )


def by_axis(array, axes):
    for axis in axes:
        array = lax.psum(array, axis)
    return array


def copy_for_each(array, axis):
    copies = jnp.broadcast_to(array, (lax.axis_size(axis), *array.shape))
    return lax.all_to_all(copies, axis, split_axis=0, concat_axis=0, tiled=True)


def over_copies(array, axis):
    everything = copy_for_each(array, axis)
    return jnp.sum(everything, axis=0)


def project(basis_f32, gram):
    return jnp.einsum(
        "hcdr,hcde,hces->hcrs", basis_f32, gram, basis_f32, precision=lax.Precision.HIGHEST
    )


def body(queries, keys, values, segments, basis):
    tok_rows = queries.shape[0]
    local_heads = keys.shape[1] // HD
    per_group = QH // KVH
    cycle_index = lax.axis_index(SEQ)
    cycle_size = lax.axis_size(SEQ)
    query_heads = queries.reshape(tok_rows, local_heads, per_group, HD)
    query_pos = cycle_index * tok_rows + jnp.arange(tok_rows, dtype=jnp.int32)
    seg_here = segments.astype(jnp.float32)
    score_scale = float(HD) ** (-0.5)
    initial = (
        jnp.full((local_heads, per_group, tok_rows), -1e30, jnp.float32),
        jnp.zeros((local_heads, per_group, tok_rows), jnp.float32),
        jnp.zeros((local_heads, per_group, tok_rows, HD), jnp.float32),
    )
    seg_wire = segments.astype(jnp.bfloat16)
    carried = initial
    usable = True
    key_block, value_block, seg_block = sent_together((keys, values, seg_wire), SEQ, 0, 1)
    key_count = key_block.shape[0]
    key_width = min(key_count, 512)
    part_count = key_count // key_width
    key_parts = key_block.reshape(part_count, key_width, local_heads, HD)
    value_parts = value_block.reshape(part_count, key_width, local_heads, HD)
    seg_parts = seg_block.reshape(part_count, key_width)
    usable = jnp.asarray(usable)

    def one_part(carried, inputs):
        key_part, value_part, seg_part, number = inputs
        first_key = number * key_width
        key_pos = first_key + jnp.arange(key_width, dtype=jnp.int32)
        seg_keys = seg_part.astype(jnp.float32)
        running_max, running_sum, weighted = carried
        allowed = (
            (key_pos[None, :] <= query_pos[:, None])
            & (seg_keys[None, :] == seg_here[:, None])
            & usable
        )
        scores = (
            jnp.einsum("tgjd,sgd->gjts", query_heads, key_part, preferred_element_type=jnp.float32)
            * score_scale
        )
        scores = jnp.where(allowed[None, None], scores, -1e30)
        new_max = jnp.maximum(running_max, jnp.max(scores, axis=-1))
        weights = jnp.where(allowed[None, None], jnp.exp(scores - new_max[..., None]), 0.0)
        factor = jnp.exp(running_max - new_max)
        running_sum = running_sum * factor + jnp.sum(weights, axis=-1)
        weighted = weighted * factor[..., None] + jnp.einsum(
            "gjts,sgd->gjtd",
            weights.astype(jnp.bfloat16),
            value_part,
            preferred_element_type=jnp.float32,
        )
        carried = (new_max, running_sum, weighted)
        return (carried, None)

    carried, unused = lax.scan(
        one_part,
        carried,
        (key_parts, value_parts, seg_parts, jnp.arange(part_count, dtype=jnp.int32)),
    )
    running_max, running_sum, weighted = carried
    mixed = weighted / running_sum[..., None]
    attention = (
        jnp.transpose(mixed, (2, 0, 1, 3))
        .astype(jnp.bfloat16)
        .reshape(tok_rows, local_heads * per_group * HD)
    )
    key_heads = keys.reshape(tok_rows, local_heads, HD)
    value_heads = values.reshape(tok_rows, local_heads, HD)
    gram_local = jnp.stack(
        [
            jnp.einsum("tgd,tge->gde", key_heads, key_heads, preferred_element_type=jnp.float32),
            jnp.einsum(
                "tgd,tge->gde", value_heads, value_heads, preferred_element_type=jnp.float32
            ),
        ],
        axis=1,
    )
    basis_f32 = basis.astype(jnp.float32)
    all_tokens = tok_rows * cycle_size
    seen_local = project(basis_f32, gram_local)
    energy_local = jnp.trace(gram_local, axis1=2, axis2=3)
    seen, energy = (by_axis(seen_local, SEQ), by_axis(energy_local, SEQ))
    captured = seen / all_tokens
    energy_total = over_copies(jnp.sum(energy, axis=0), "kvh")
    share = KVH * energy / energy_total[None, :]
    key_lat = jnp.einsum("tgd,gdr->tgr", key_heads, basis[:, 0], preferred_element_type=jnp.float32)
    value_lat = jnp.einsum(
        "tgd,gdr->tgr", value_heads, basis[:, 1], preferred_element_type=jnp.float32
    )
    latents = (
        jnp.concatenate([key_lat, value_lat], axis=-1)
        .astype(jnp.bfloat16)
        .reshape(tok_rows, local_heads * 2 * RANK)
    )
    return (attention, latents, captured, share)


def solution(mesh):
    torus = Mesh(
        mesh.devices.reshape(2, 8, 4, mesh.shape["kvh"]), ("seq_0", "seq_1", "seq_2", "kvh")
    )
    in_specs = (P(SEQ, "kvh"), P(SEQ, "kvh"), P(SEQ, "kvh"), P(SEQ), P("kvh", None, None, None))
    out_specs = (P(SEQ, "kvh"), P(SEQ, "kvh"), P("kvh", None, None, None), P("kvh", None))
    return jax.shard_map(body, mesh=torus, in_specs=in_specs, out_specs=out_specs, check_vma=False)
```

profile of v0, /device:TPU:1, one launch (start us, length us, event | category | flops | bytes accessed | tf_op | source)
XLA Modules:
  0.0 312.1 jit_solution(9679736985981669802)
XLA Ops:
  8.1 1.6 pad_maximum_fusion.1
  9.7 1.1 convolution_bitcast_fusion.1
  10.8 1.1 convolution_bitcast_fusion
  12.1 1.0 fusion.19
  14.0 10.7 %all-reduce.2 = (f32[2,2,32,32]{3,2,1,0:T(8,128)S(1)}, f32[2,2]{0,1:T(2,128)S(1)}) all-reduce(f32[2,2,32,32]{3,2,1,0:T(8,128)S(1)} %fusion.35, f32[2,2]{0,1:T(2,128)S(1)} %get-tuple-element.203), channel_id=1, replica_groups=mesh['seq_0'=2,'seq_1'=8,'seq_2'=4,'kvh'=4] {'seq_0'}, use_global_device_ids=true, to_apply=%region_4.5 | all-reduce | flops 4100 | bytes 32800 | tf_op jit(solution)/shard_map/psum | solution.py:30
  24.7 27.5 %all-reduce = (f32[2,2,32,32]{3,2,1,0:T(8,128)S(1)}, f32[2,2]{0,1:T(2,128)S(1)}) all-reduce(f32[2,2,32,32]{3,2,1,0:T(8,128)S(1)} %get-tuple-element.193, f32[2,2]{0,1:T(2,128)S(1)} %get-tuple-element.194), channel_id=1, replica_groups=mesh['seq_0'=2,'seq_1'=8,'seq_2'=4,'kvh'=4] {'seq_1'}, use_global_device_ids=true, to_apply=%region_5.6 | all-reduce | flops 4100 | bytes 32800 | tf_op jit(solution)/shard_map/psum | solution.py:30
  52.2 14.0 %all-reduce.1 = (f32[2,2,32,32]{3,2,1,0:T(8,128)S(1)}, f32[2,2]{0,1:T(2,128)S(1)}) all-reduce(f32[2,2,32,32]{3,2,1,0:T(8,128)S(1)} %get-tuple-element.189, f32[2,2]{0,1:T(2,128)S(1)} %get-tuple-element.190), channel_id=1, replica_groups=mesh['seq_0'=2,'seq_1'=8,'seq_2'=4,'kvh'=4] {'seq_2'}, use_global_device_ids=true, to_apply=%region_6.7 | all-reduce | flops 4100 | bytes 32800 | tf_op jit(solution)/shard_map/psum | solution.py:30
  66.9 16.4 %all-to-all-start = ((f32[4,1,2]{2,1,0:T(1,128)}), f32[4,1,2]{2,1,0:T(1,128)S(1)}, u32[]{:S(2)}, u32[]{:S(2)}) async-start(f32[4,1,2]{2,1,0:T(1,128)} %broadcast_in_dim.54), calls=%async_computation | async-start | bytes 4096 | tf_op jit(solution)/shard_map/all_to_all | solution.py:36
  84.3 1.0 fusion.17
  86.1 1.3 copy.82
  89.1 89.2 %all-gather.2.cloned.1.call-done = bf16[8192,513]{1,0:T(8,128)(2,1)} async-done(((bf16[128,513]{1,0:T(8,128)(2,1)}), bf16[8192,513]{1,0:T(8,128)(2,1)}) %all-gather.2.cloned.1.call-update) | async-done | bytes 8405008 | tf_op jit(solution)/shard_map/all_gather | solution.py:21
  178.3 5.8 %fusion.33 = (bf16[8192,256]{1,0:T(8,128)(2,1)}, bf16[8192,256]{1,0:T(8,128)(2,1)}) fusion(bf16[8192,513]{1,0:T(8,128)(2,1)} %all-gather.2.cloned.1.call-done), kind=kLoop, calls=%fused_computation.58 | loop fusion | bytes 16777216 | tf_op jit(solution)/shard_map/split | solution.py:22
  184.1 6.9 %reshape.114 = bf16[16,512,2,128]{3,2,1,0:T(2,128)(2,1)} reshape(bf16[8192,256]{1,0:T(8,128)(2,1)} %get-tuple-element.201) | data formatting | bytes 8388608 | tf_op jit(solution)/shard_map/reshape | solution.py:73
  191.1 2.2 slice_reduce_fusion
  193.3 6.9 %reshape.113 = bf16[16,512,2,128]{3,2,1,0:T(2,128)(2,1)} reshape(bf16[8192,256]{1,0:T(8,128)(2,1)} %get-tuple-element.202) | data formatting | bytes 8388608 | tf_op jit(solution)/shard_map/reshape | solution.py:72
  200.2 103.3 %while.15 = (s32[]{:T(128)}, f32[2,8,128]{2,1,0:T(8,128)S(1)}, f32[2,8,128]{2,1,0:T(8,128)S(1)}, f32[2,8,128,128]{3,2,1,0:T(8,128)S(1)}, s32[16]{0:T(128)S(1)}, ...) while((s32[]{:T(128)}, f32[2,8,128]{2,1,0:T(8,128)S(1)}, ...), condition=%wide.region_3.4_spmd.clone, body=%wide.region_0.3_spmd.clone.sunk | while | flops 551496832 | bytes 17181376 | solution.py:106
  201.7 1.4 constant_dynamic-slice_fusion.3
  205.0 1.7 fusion.55
  208.2 1.4 constant_dynamic-slice_fusion.3
  211.4 1.7 fusion.55
  214.7 1.4 constant_dynamic-slice_fusion.3
  217.9 1.7 fusion.55
  221.1 1.4 constant_dynamic-slice_fusion.3
  224.3 1.7 fusion.55
  227.6 1.4 constant_dynamic-slice_fusion.3
  230.8 1.7 fusion.55
  234.0 1.4 constant_dynamic-slice_fusion.3
  237.3 1.7 fusion.55
  240.5 1.4 constant_dynamic-slice_fusion.3
  243.7 1.7 fusion.55
  247.0 1.4 constant_dynamic-slice_fusion.3
  250.2 1.7 fusion.55
  253.4 1.4 constant_dynamic-slice_fusion.3
  256.6 1.7 fusion.55
  259.9 1.4 constant_dynamic-slice_fusion.3
  263.1 1.7 fusion.55
  266.3 1.4 constant_dynamic-slice_fusion.3
  269.5 1.7 fusion.55
  272.8 1.4 constant_dynamic-slice_fusion.3
  276.0 1.7 fusion.55
  279.2 1.4 constant_dynamic-slice_fusion.3
  282.5 1.7 fusion.55
  285.7 1.4 constant_dynamic-slice_fusion.3
  288.9 1.7 fusion.55
  292.2 1.4 constant_dynamic-slice_fusion.3
  295.4 1.7 fusion.55
  298.6 1.4 constant_dynamic-slice_fusion.3
  301.8 1.7 fusion.55
  (186 shorter events, 49.4 us)
Async XLA Ops:
  7.2 171.2 %all-gather.2.cloned.1.call-start = ((), (), s32[]{:S(2)}) async-start(), calls=%async_computation.1 | async-start | bytes 10649600 | tf_op jit(solution)/shard_map/all_gather | solution.py:21
  66.9 21.4 %all-to-all-start = ((f32[4,1,2]{2,1,0:T(1,128)}), f32[4,1,2]{2,1,0:T(1,128)S(1)}, u32[]{:S(2)}, u32[]{:S(2)}) async-start(f32[4,1,2]{2,1,0:T(1,128)} %broadcast_in_dim.54), calls=%async_computation | async-start | bytes 4096 | tf_op jit(solution)/shard_map/all_to_all | solution.py:36
Sparse Core Ops, SparseCore 0:
  12.2 166.1 all-gather.1
where the time goes:
time: 313 us; the launch traced here: 312 us
  waiting for transfers between devices  89.3 us (29%)
  local copies, waits for them, and re-layouts  58.7 us (19%)
  blocking collectives  52.2 us (17%)
  matrix products  45.8 us (15%)
  other arithmetic  23.7 us (8%)
  starting transfers between devices  16.5 us (5%)
  between operations  14.1 us (5%)
  loops' own time  11.9 us (4%)
    all_gather x1, waiting for transfers between devices, sent_together(): result = lax.all_gather(both, axis, axis=dim, tiled=True)  89.2 us
    psum x3, blocking collectives, by_axis(): array = lax.psum(array, axis)  52.2 us
    dynamic_slice x32, local copies, waits for them, and re-layouts, body(): lax.scan(one_part, carried, (key_parts, value_parts, seg_parts, jnp.arang...  31.7 us
    dot_general x16, matrix products, one_part(): jnp.einsum('gjts,sgd->gjtd', weights.astype(jnp.bfloat16), value_part, pr...  27.4 us
    all_to_all x1, starting transfers between devices, copy_for_each(): return lax.all_to_all(copies, axis, split_axis=0, concat_axis=0, tiled=True)  16.4 us
    reduce_sum x16, other arithmetic, one_part(): running_sum = running_sum * factor + jnp.sum(weights, axis=-1)  16 us
    dot_general x16, matrix products, one_part(): jnp.einsum('tgjd,sgd->gjts', query_heads, key_part, preferred_element_typ...  12.2 us
    another operation x1, loops' own time, body(): lax.scan(one_part, carried, (key_parts, value_parts, seg_parts, jnp.arang...  11.9 us
  transfers between devices with their start and end apart: 2, of which 1 were waited for; matrix products, arithmetic and copies ran while one was open for 3% of the time, Pallas kernels for 0%

commit v1 on v0

v1 whole, which is shorter than its diff:
```python
import functools
import math

import jax
import jax.numpy as jnp
from jax import lax
from jax.experimental import pallas as pl
from jax.experimental.pallas import tpu as pltpu
from jax.sharding import Mesh
from jax.sharding import PartitionSpec as P

HD = 128
QH = 64
KVH = 8
RANK = 32
TOKENS = 8192
SLABS = 16
SEQ = ("a", "z", "y")
KV = ("xl", "c")
RING = ("a", "z")
COLUMN = ("y", "c")
BLOCK = 144
HALF = 2 * BLOCK
SCALE2 = HD**-0.5 * math.log2(math.e)
FIRST = -1e30
MASKED = -2e30
FAR = 1e9

GROUPS = ((0, 1, 8, 2, 7), (3, 6, 4, 5))


def to_heads(t):
    pairs = []
    for y in range(4):
        for c in range(2):
            head = (y & 1) ^ t
            pairs.append((y * 2 + c, (2 * c + head) * 2 + (y >> 1)))
    return pairs


def shifted(array, by):
    return lax.ppermute(array, RING, [(i, (i + by) % SLABS) for i in range(SLABS)])


def added(array, axis, distance):
    size = lax.axis_size(axis)
    return array + lax.ppermute(array, axis, [(i, i ^ distance) for i in range(size)])


def local_kernel(where_ref, keys_ref, values_ref, basis_ref, latents_ref, stats_ref):
    kvh = where_ref[0]
    lane = lax.broadcasted_iota(jnp.int32, (8, 128), 1)
    projected = []
    energies = jnp.zeros((8, 128), jnp.float32)
    for g in range(2):
        for kind, ref in enumerate((keys_ref, values_ref)):
            rows = ref[:, g * HD : (g + 1) * HD]
            projected.append(
                jnp.dot(rows, basis_ref[g, kind], preferred_element_type=jnp.float32)
            )
            squares = rows.astype(jnp.float32)
            total = jnp.sum(squares * squares)
            energies = jnp.where(lane == kvh * 4 + g * 2 + kind, total, energies)
    latents = jnp.concatenate(projected, axis=1)
    latents_ref[...] = latents.astype(jnp.bfloat16)
    seen = lax.dot_general(
        latents,
        latents,
        (((0,), (0,)), ((), ())),
        precision=lax.Precision.HIGHEST,
        preferred_element_type=jnp.float32,
    )
    wide = lax.broadcasted_iota(jnp.int32, (RANK, 128), 1) // RANK
    packed = jnp.zeros((RANK, 128), jnp.float32)
    for n in range(4):
        packed = jnp.where(wide == n, seen[n * RANK : (n + 1) * RANK, :], packed)
    row = lax.broadcasted_iota(jnp.int32, (8, 128), 0)
    stats_ref[0:RANK, :] = packed
    stats_ref[RANK : RANK + 8, :] = jnp.where(row == 0, energies, 0.0)


def attend_kernel(count, tail, first, last, *refs):
    refs = list(refs)
    where_ref, q0_ref, q1_ref, mine_ref, theirs_ref = refs[:5]
    refs = refs[5:]
    if not first:
        starts_in, top_in, sum_in, mix_in = refs[:4]
        refs = refs[4:]
    if last:
        out_refs = refs[:2]
        starts_ref, top_ref, sum_ref, mix_ref = refs[2:]
    else:
        starts_ref, top_ref, sum_ref, mix_ref = refs
    slab, core, odd = where_ref[0], where_ref[1], where_ref[2]

    def pieces(i, with_tail):
        at = where_ref[3 + i] * 512
        found = []
        for ref, half in ((mine_ref, core), (theirs_ref, 1 - core)):
            if with_tail:
                found.append((ref, i * HALF, at + half * 256 + 128))
            else:
                for t in range(2):
                    found.append((ref, i * HALF + t * BLOCK, at + half * 256 + (odd ^ t) * 128))
        return found

    if first:
        one = jnp.full((16, 128), FAR, jnp.float32)
        two = one
    else:
        one = starts_in[0:16, :]
        two = starts_in[16:32, :]
    for i in range(count + int(tail)):
        for ref, row, base in pieces(i, i == count):
            counts = ref[row + 128 : row + BLOCK, :].astype(jnp.float32)
            at = base.astype(jnp.float32)
            n1, n2 = counts[:, :128], counts[:, 128:]
            one = jnp.minimum(one, jnp.where(n1 < 128.0, at + n1, FAR))
            two = jnp.minimum(two, jnp.where(n2 < 128.0, at + n2, FAR))
    starts_ref[0:16, :] = one
    starts_ref[16:32, :] = two
    start1 = jnp.min(one).astype(jnp.int32)
    start2 = jnp.min(two).astype(jnp.int32)

    if first:
        top_ref[...] = jnp.full(top_ref.shape, FIRST, jnp.float32)
        sum_ref[...] = jnp.zeros(sum_ref.shape, jnp.float32)
        mix_ref[...] = jnp.zeros(mix_ref.shape, jnp.float32)
    else:
        top_ref[...] = top_in[...]
        sum_ref[...] = sum_in[...]
        mix_ref[...] = mix_in[...]

    q_base = [slab * 512 + core * 256 + (odd ^ t) * 128 for t in range(2)]
    row_iota = lax.broadcasted_iota(jnp.int32, (128, 128), 0)
    lane_iota = lax.broadcasted_iota(jnp.int32, (128, 128), 1)

    def slab_step(i, with_tail):
        found = pieces(i, with_tail)
        at = where_ref[3 + i] * 512
        for t, q_ref in enumerate((q0_ref, q1_ref)):
            low = jnp.where(
                q_base[t] >= start2, start2, jnp.where(q_base[t] >= start1, start1, 0)
            )
            needed = (at <= q_base[t] + 127) & (at + 511 >= low)

            @pl.when(needed)
            def _(t=t, q_ref=q_ref):
                q_pos = q_base[t] + row_iota
                lows = jnp.where(
                    q_pos >= start2, start2, jnp.where(q_pos >= start1, start1, 0)
                )
                allowed, k_parts, v_parts = [], [], []
                for ref, row, base in found:
                    k_pos = base + lane_iota
                    allowed.append((k_pos >= lows) & (k_pos <= q_pos))
                    rows = pl.ds(row, 128) if isinstance(row, int) else pl.ds(pl.multiple_of(row, 16), 128)
                    k_parts.append(ref[rows, 0:HD])
                    v_parts.append(ref[rows, HD : 2 * HD])
                k = jnp.concatenate(k_parts, axis=0)
                v = jnp.concatenate(v_parts, axis=0)
                for pair in range(4):
                    heads = (2 * pair, 2 * pair + 1)
                    q = jnp.concatenate([q_ref[:, j * HD : (j + 1) * HD] for j in heads], axis=0)
                    scores = lax.dot_general(
                        q, k, (((1,), (1,)), ((), ())), preferred_element_type=jnp.float32
                    )
                    parts = []
                    for n, mask in enumerate(allowed):
                        mask2 = jnp.concatenate([mask, mask], axis=0)
                        parts.append(
                            jnp.where(mask2, scores[:, n * 128 : (n + 1) * 128], MASKED)
                        )
                    best = functools.reduce(jnp.maximum, parts)
                    span = slice(t * 1024 + pair * 256, t * 1024 + pair * 256 + 256)
                    top_old = top_ref[span, :]
                    top = jnp.maximum(top_old, jnp.max(best, axis=1, keepdims=True))
                    factor = jnp.exp2((top_old - top) * SCALE2)
                    weights = [jnp.exp2((part - top) * SCALE2) for part in parts]
                    sum_ref[span, :] = sum_ref[span, :] * factor + functools.reduce(
                        jnp.add, weights
                    )
                    rounded = jnp.concatenate([w.astype(jnp.bfloat16) for w in weights], axis=1)
                    mix_ref[span, :] = mix_ref[span, :] * factor + jnp.dot(
                        rounded, v, preferred_element_type=jnp.float32
                    )
                    top_ref[span, :] = top

    def loop_step(i, carry):
        slab_step(i, False)
        return carry

    lax.fori_loop(0, count, loop_step, 0)
    if tail:
        slab_step(count, True)
    if last:
        for t in range(2):
            for j in range(8):
                span = slice(t * 1024 + j * 128, t * 1024 + (j + 1) * 128)
                total = jnp.sum(sum_ref[span, :], axis=1, keepdims=True)
                out_refs[t][:, j * HD : (j + 1) * HD] = (mix_ref[span, :] / total).astype(
                    jnp.bfloat16
                )


def vmem():
    return pl.BlockSpec(memory_space=pltpu.VMEM)


def attend(where, q0, q1, mine, theirs, state, count, tail, last):
    first = state is None
    carry = [
        jax.ShapeDtypeStruct((32, 128), jnp.float32),
        jax.ShapeDtypeStruct((2048, 128), jnp.float32),
        jax.ShapeDtypeStruct((2048, 128), jnp.float32),
        jax.ShapeDtypeStruct((2048, 128), jnp.float32),
    ]
    keys = count * 512 + (256 if tail else 0)
    cost = pl.CostEstimate(
        flops=4 * 2048 * keys * HD, bytes_accessed=4 * 1024 * 1024, transcendentals=2048 * keys
    )
    if last:
        out_shape = [jax.ShapeDtypeStruct((128, 1024), jnp.bfloat16)] * 2
        scratch = [pltpu.VMEM(c.shape, c.dtype) for c in carry]
    else:
        out_shape, scratch = carry, []
    inputs = [q0, q1, mine, theirs] + ([] if first else list(state))
    return pl.pallas_call(
        functools.partial(attend_kernel, count, tail, first, last),
        out_shape=out_shape,
        in_specs=[pl.BlockSpec(memory_space=pltpu.SMEM)] + [vmem()] * len(inputs),
        out_specs=[vmem()] * len(out_shape),
        scratch_shapes=scratch,
        compiler_params=pltpu.CompilerParams(vmem_limit_bytes=24 * 1024 * 1024),
        cost_estimate=cost,
        name="attend_last" if last else "attend",
    )(where, *inputs)


def body(queries, keys, values, segments, basis):
    a, z, y = lax.axis_index("a"), lax.axis_index("z"), lax.axis_index("y")
    c, xl = lax.axis_index("c"), lax.axis_index("xl")
    odd = y & 1
    kvh = xl * 2 + c
    slab = a * 8 + z

    n1 = jnp.sum((segments < 1).astype(jnp.float32))
    n2 = jnp.sum((segments < 2).astype(jnp.float32))
    lanes = lax.broadcasted_iota(jnp.int32, (16, 256), 1)
    counts = jnp.where(lanes < 128, n1, n2).astype(jnp.bfloat16)

    def block_of(head):
        return jnp.concatenate(
            [
                jnp.concatenate(
                    [
                        lax.dynamic_slice_in_dim(keys, head * HD, HD, 1),
                        lax.dynamic_slice_in_dim(values, head * HD, HD, 1),
                    ],
                    axis=1,
                ),
                counts,
            ],
            axis=0,
        )

    kv = [lax.ppermute(block_of(odd ^ t), COLUMN, to_heads(t)) for t in range(2)]
    q = [
        lax.ppermute(
            lax.dynamic_slice_in_dim(queries, (odd ^ t) * 1024, 1024, 1), COLUMN, to_heads(t)
        )
        for t in range(2)
    ]

    at = {0: jnp.concatenate(kv, axis=0)}
    at[1] = shifted(at[0], 1)
    at[8] = shifted(at[0], 8)
    at[2] = shifted(at[1], 1)
    at[7] = shifted(at[8], -1)
    tail = shifted(jnp.where(odd == 0, at[8][BLOCK:], at[8][:BLOCK]), 1)
    at[3] = shifted(at[2], 1)
    at[6] = shifted(at[7], -1)
    at[4] = shifted(at[3], 1)
    at[5] = shifted(at[6], -1)

    latents, stats = pl.pallas_call(
        local_kernel,
        out_shape=[
            jax.ShapeDtypeStruct((128, 128), jnp.bfloat16),
            jax.ShapeDtypeStruct((RANK + 8, 128), jnp.float32),
        ],
        in_specs=[pl.BlockSpec(memory_space=pltpu.SMEM)] + [vmem()] * 3,
        out_specs=[vmem()] * 2,
        cost_estimate=pl.CostEstimate(
            flops=1 << 26, bytes_accessed=1 << 18, transcendentals=0
        ),
        name="local",
    )(kvh.reshape(1), keys, values, basis)

    state = None
    for n, group in enumerate(GROUPS):
        last = n == len(GROUPS) - 1
        mine = [at[d] for d in group] + ([tail] if last else [])
        mine = jnp.concatenate(mine, axis=0)
        theirs = lax.ppermute(mine, "c", [(0, 1), (1, 0)])
        distances = list(group) + ([9] if last else [])
        where = jnp.stack([slab, c, odd] + [(slab - d) % SLABS for d in distances])
        where = where.astype(jnp.int32)
        state = attend(where, q[0], q[1], mine, theirs, state, len(group), last, last)

    back = [
        lax.ppermute(state[t], COLUMN, [(d, s) for s, d in to_heads(t)]) for t in range(2)
    ]
    attention = jnp.where(
        odd == 0, jnp.concatenate(back, axis=1), jnp.concatenate(back[::-1], axis=1)
    )

    for axis, distance in (("y", 1), ("y", 2), ("z", 1), ("z", 2), ("z", 4), ("a", 1)):
        stats = added(stats, axis, distance)
    seen = stats[:RANK].reshape(RANK, 4, RANK).transpose(1, 0, 2).reshape(2, 2, RANK, RANK)
    captured = seen / TOKENS
    energies = added(added(stats[RANK:], "c", 1), "xl", 1)[0, : 2 * KVH].reshape(KVH, 2)
    own = lax.dynamic_slice_in_dim(energies, kvh * 2, 2, 0)
    share = KVH * own / jnp.sum(energies, axis=0)[None, :]
    return (attention, latents, captured, share)


def solution(mesh):
    torus = Mesh(mesh.devices.reshape(2, 8, 4, 2, 2), ("a", "z", "y", "xl", "c"))
    in_specs = (P(SEQ, KV), P(SEQ, KV), P(SEQ, KV), P(SEQ), P(KV, None, None, None))
    out_specs = (P(SEQ, KV), P(SEQ, KV), P(KV, None, None, None), P(KV, None))
    return jax.shard_map(body, mesh=torus, in_specs=in_specs, out_specs=out_specs, check_vma=False)
```

time: 313 us -> 122 us (0.39)
  the two profiles are of different devices: /device:TPU:1 before, /device:TPU:231 now
where the time goes in v1:
time: 122 us
  starting transfers between devices  52.8 us (43%)
  Pallas kernels  30.2 us (25%)
  waiting for transfers between devices  29.7 us (24%)
  other arithmetic  4.21 us (3%)
  local copies, waits for them, and re-layouts  4.19 us (3%)
    pallas_call x2, Pallas kernels, attend(): pl.pallas_call(functools.partial(attend_kernel, count, tail, first, last)...  28 us
    ppermute x9, starting transfers between devices, shifted(): lax.ppermute(array, RING, [(i, (i + by) % SLABS) for i in range(SLABS)])  21.1 us
    ppermute x9, waiting for transfers between devices, shifted(): lax.ppermute(array, RING, [(i, (i + by) % SLABS) for i in range(SLABS)])  11.6 us
    ppermute x8, waiting for transfers between devices, added(): lax.ppermute(array, axis, [(i, i ^ distance) for i in range(size)])  10.8 us
    ppermute x2, starting transfers between devices, body(): lax.ppermute(block_of(odd ^ t), COLUMN, to_heads(t))  8.46 us
    ppermute x2, starting transfers between devices, body(): lax.ppermute(lax.dynamic_slice_in_dim(queries, (odd ^ t) * 1024, 1024, 1)...  7.37 us
    ppermute x2, waiting for transfers between devices, body(): lax.ppermute(state[t], COLUMN, [(d, s) for s, d in to_heads(t)])  7.32 us
    ppermute x2, starting transfers between devices, body(): theirs = lax.ppermute(mine, 'c', [(0, 1), (1, 0)])  6.14 us
  transfers between devices with their start and end apart: 25, of which 12 were waited for; matrix products, arithmetic and copies ran while one was open for 3% of the time, Pallas kernels for 14%

profile of v1, /device:TPU:231, one launch (start us, length us, event | category | flops | bytes accessed | tf_op | source)
XLA Modules:
  0.0 122.1 jit_solution(11978117585693264892)
XLA Ops:
  0.7 0.6 copy-done.2
  1.3 0.6 fusion.3
  1.9 1.3 %fusion.2 = bf16[256]{0:T(256)(128)(2,1)S(1)} fusion(bf16[]{:T(256)} %get-tuple-element.21, bf16[]{:T(256)} %get-tuple-element.20), kind=kLoop, calls=%fused_computation.30 | loop fusion | flops 512 | bytes 516 | tf_op jit(solution)/shard_map/convert_element_type | solution.py:250
  3.2 0.8 constant_dynamic-slice_fusion.1
  4.1 5.4 %collective-permute-start.2 = (bf16[144,256]{1,0:T(8,128)(2,1)S(1)}, bf16[144,256]{1,0:T(8,128)(2,1)S(1)}, u32[]{:S(2)}, u32[]{:S(2)}) collective-permute-start(bf16[144,256]{1,0:T(8,128)(2,1)S(1)} %get-tuple-element.33), channel_id=1, source_target_pairs={{0,0},{1,8},{4,4},{5,12},{8,1},{9,9},{12,5},{13,13},{2,2},{3,10},{... | collective-permute-start | bytes 221192 | tf_op jit(solution)/shard_map/ppermute | solution.py:267
  9.5 0.8 copy.11.basis_ref
  10.3 2.2 %local.1 = (bf16[128,128]{1,0:T(8,128)(2,1)}, f32[40,128]{1,0:T(8,128)}) custom-call(s32[1]{0:T(128)} %bitcast.13.where_ref, bf16[128,256]{1,0:T(8,128)(2,1)} %keys_ref.1, bf16[128,256]{1,0:T(8,128)(2,1)} %values_ref.1, bf16[2,2,128,32]{3,2,1,0:T(8,128)(2,1)} %copy.11.basis_ref), custom_call_target="tpu_custom_call" | custom-call | flops 67108864 | bytes 262144 | tf_op jit(solution)/shard_map/local/pallas_call | solution.py:286
  12.4 0.4 collective-permute-start.17
  12.8 2.4 %collective-permute-done.17 = f32[40,128]{1,0:T(8,128)S(1)} collective-permute-done((f32[40,128]{1,0:T(8,128)}, f32[40,128]{1,0:T(8,128)S(1)}, u32[]{:S(2)}, u32[]{:S(2)}) %collective-permute-start.17) | collective-permute-done | bytes 20512 | tf_op jit(solution)/shard_map/ppermute | solution.py:47
  15.3 0.7 add.103
  16.0 4.1 %collective-permute-done.18 = f32[40,128]{1,0:T(8,128)S(1)} collective-permute-done((f32[40,128]{1,0:T(8,128)S(1)}, f32[40,128]{1,0:T(8,128)S(1)}, u32[]{:S(2)}, u32[]{:S(2)}) %collective-permute-start.18) | collective-permute-done | bytes 20512 | tf_op jit(solution)/shard_map/ppermute | solution.py:47
  20.2 0.7 collective-permute-start.19
  20.9 3.1 %collective-permute-start.3 = (bf16[144,256]{1,0:T(8,128)(2,1)S(1)}, bf16[144,256]{1,0:T(8,128)(2,1)S(1)}, u32[]{:S(2)}, u32[]{:S(2)}) collective-permute-start(bf16[144,256]{1,0:T(8,128)(2,1)S(1)} %get-tuple-element.32), channel_id=1, source_target_pairs={{0,4},{1,12},{4,0},{5,8},{8,5},{9,13},{12,1},{13,9},{2,6},{3,14},{... | collective-permute-start | bytes 221192 | tf_op jit(solution)/shard_map/ppermute | solution.py:267
  24.0 1.3 %collective-permute-start.20 = (f32[40,128]{1,0:T(8,128)S(1)}, f32[40,128]{1,0:T(8,128)S(1)}, u32[]{:S(2)}, u32[]{:S(2)}) collective-permute-start(f32[40,128]{1,0:T(8,128)S(1)} %add.105), channel_id=1, source_target_pairs={{0,32},{16,48},{32,0},{48,16},{64,96},{80,112},{96,64},{112,80},{1... | collective-permute-start | bytes 61448 | tf_op jit(solution)/shard_map/ppermute | solution.py:47
  25.2 2.5 %collective-permute-done.20 = f32[40,128]{1,0:T(8,128)S(1)} collective-permute-done((f32[40,128]{1,0:T(8,128)S(1)}, f32[40,128]{1,0:T(8,128)S(1)}, u32[]{:S(2)}, u32[]{:S(2)}) %collective-permute-start.20) | collective-permute-done | bytes 20512 | tf_op jit(solution)/shard_map/ppermute | solution.py:47
  27.8 0.3 collective-permute-start.21
  28.1 4.7 %collective-permute-start.4 = (bf16[288,256]{1,0:T(8,128)(2,1)S(1)}, bf16[288,256]{1,0:T(8,128)(2,1)S(1)}, u32[]{:S(2)}, u32[]{:S(2)}) collective-permute-start(bf16[288,256]{1,0:T(8,128)(2,1)S(1)} %get-tuple-element.25), channel_id=1, source_target_pairs={{0,16},{16,32},{32,48},{48,64},{64,80},{80,96},{96,112},{112,128},... | collective-permute-start | bytes 442376 | tf_op jit(solution)/shard_map/ppermute | solution.py:42
  32.7 1.8 %collective-permute-start.7 = (bf16[288,256]{1,0:T(8,128)(2,1)S(1)}, bf16[288,256]{1,0:T(8,128)(2,1)S(1)}, u32[]{:S(2)}, u32[]{:S(2)}) collective-permute-start(bf16[288,256]{1,0:T(8,128)(2,1)S(1)} %get-tuple-element.25), channel_id=1, source_target_pairs={{0,128},{16,144},{32,160},{48,176},{64,192},{80,208},{96,224},{112... | collective-permute-start | bytes 442376 | tf_op jit(solution)/shard_map/ppermute | solution.py:42
  34.6 1.2 collective-permute-start.22
  35.8 0.8 constant_dynamic-slice_fusion.5
  36.6 6.4 %collective-permute-start = (bf16[128,1024]{1,0:T(8,128)(2,1)}, bf16[128,1024]{1,0:T(8,128)(2,1)S(1)}, u32[]{:S(2)}, u32[]{:S(2)}) collective-permute-start(bf16[128,1024]{1,0:T(8,128)(2,1)} %get-tuple-element.23), channel_id=1, source_target_pairs={{0,0},{1,8},{4,4},{5,12},{8,1},{9,9},{12,5},{13,13},{2,2},{3,10},{... | collective-permute-start | bytes 786440 | tf_op jit(solution)/shard_map/ppermute | solution.py:269
  43.0 1.0 collective-permute-start.1
  44.1 0.1 stack.56.refs_0_
  44.2 0.1 collective-permute-start.23
  44.3 0.3 collective-permute-start.5
  44.7 1.2 collective-permute-start.8
  45.9 3.5 %collective-permute-done.5 = bf16[288,256]{1,0:T(8,128)(2,1)S(1)} collective-permute-done((bf16[288,256]{1,0:T(8,128)(2,1)S(1)}, bf16[288,256]{1,0:T(8,128)(2,1)S(1)}, u32[]{:S(2)}, u32[]{:S(2)}) %collective-permute-start.5) | collective-permute-done | bytes 147488 | tf_op jit(solution)/shard_map/ppermute | solution.py:42
  49.4 4.0 %collective-permute-start.6 = (bf16[288,256]{1,0:T(8,128)(2,1)S(1)}, bf16[288,256]{1,0:T(8,128)(2,1)S(1)}, u32[]{:S(2)}, u32[]{:S(2)}) collective-permute-start(bf16[288,256]{1,0:T(8,128)(2,1)S(1)} %collective-permute-done.5), channel_id=1, source_target_pairs={{0,16},{16,32},{32,48},{48,64},{64,80},{80,96},{96,112},{112,128},... | collective-permute-start | bytes 442376 | tf_op jit(solution)/shard_map/ppermute | solution.py:42
  53.5 2.0 %collective-permute-done.6 = bf16[288,256]{1,0:T(8,128)(2,1)S(1)} collective-permute-done((bf16[288,256]{1,0:T(8,128)(2,1)S(1)}, bf16[288,256]{1,0:T(8,128)(2,1)S(1)}, u32[]{:S(2)}, u32[]{:S(2)}) %collective-permute-start.6) | collective-permute-done | bytes 147488 | tf_op jit(solution)/shard_map/ppermute | solution.py:42
  55.5 5.5 %collective-permute-start.10 = (bf16[288,256]{1,0:T(8,128)(2,1)S(1)}, bf16[288,256]{1,0:T(8,128)(2,1)S(1)}, u32[]{:S(2)}, u32[]{:S(2)}) collective-permute-start(bf16[288,256]{1,0:T(8,128)(2,1)S(1)} %collective-permute-done.6), channel_id=1, source_target_pairs={{0,16},{16,32},{32,48},{48,64},{64,80},{80,96},{96,112},{112,128},... | collective-permute-start | bytes 442376 | tf_op jit(solution)/shard_map/ppermute | solution.py:42
  61.0 0.1 collective-permute-done.9
  61.1 2.0 %collective-permute-done.10 = bf16[288,256]{1,0:T(8,128)(2,1)S(1)} collective-permute-done((bf16[288,256]{1,0:T(8,128)(2,1)S(1)}, bf16[288,256]{1,0:T(8,128)(2,1)S(1)}, u32[]{:S(2)}, u32[]{:S(2)}) %collective-permute-start.10) | collective-permute-done | bytes 147488 | tf_op jit(solution)/shard_map/ppermute | solution.py:42
  63.1 3.1 %collective-permute-start.14 = (bf16[1440,256]{1,0:T(8,128)(2,1)S(1)}, bf16[1440,256]{1,0:T(8,128)(2,1)S(1)}, u32[]{:S(2)}, u32[]{:S(2)}) collective-permute-start(bf16[1440,256]{1,0:T(8,128)(2,1)S(1)} %constant_dynamic-update-slice_fusion.7.refs_3_), channel_id=1, source_target_pairs={{0,1},{1,0},{2,3},{3,2},{4,5},{5,4},{6,7},{7,6},{8,9},{9,8},{10,11... | collective-permute-start | bytes 2211848 | tf_op jit(solution)/shard_map/ppermute | solution.py:305
  66.3 2.5 %collective-permute-done.11 = bf16[288,256]{1,0:T(8,128)(2,1)S(1)} collective-permute-done((bf16[288,256]{1,0:T(8,128)(2,1)S(1)}, bf16[288,256]{1,0:T(8,128)(2,1)S(1)}, u32[]{:S(2)}, u32[]{:S(2)}) %collective-permute-start.11) | collective-permute-done | bytes 147488 | tf_op jit(solution)/shard_map/ppermute | solution.py:42
  68.7 3.4 %collective-permute-start.12 = (bf16[144,256]{1,0:T(8,128)(2,1)S(1)}, bf16[144,256]{1,0:T(8,128)(2,1)S(1)}, u32[]{:S(2)}, u32[]{:S(2)}) collective-permute-start(bf16[144,256]{1,0:T(8,128)(2,1)S(1)} %slice_select_fusion), channel_id=1, source_target_pairs={{0,16},{16,32},{32,48},{48,64},{64,80},{80,96},{96,112},{112,128},... | collective-permute-start | bytes 221192 | tf_op jit(solution)/shard_map/ppermute | solution.py:42
  72.2 1.6 %collective-permute-done.12 = bf16[144,256]{1,0:T(8,128)(2,1)S(1)} collective-permute-done((bf16[144,256]{1,0:T(8,128)(2,1)S(1)}, bf16[144,256]{1,0:T(8,128)(2,1)S(1)}, u32[]{:S(2)}, u32[]{:S(2)}) %collective-permute-start.12) | collective-permute-done | bytes 73760 | tf_op jit(solution)/shard_map/ppermute | solution.py:42
  73.8 3.0 %collective-permute-start.13 = (bf16[1296,256]{1,0:T(8,128)(2,1)S(1)}, bf16[1296,256]{1,0:T(8,128)(2,1)S(1)}, u32[]{:S(2)}, u32[]{:S(2)}) collective-permute-start(bf16[1296,256]{1,0:T(8,128)(2,1)S(1)} %constant_dynamic-update-slice_fusion.2.refs_3_), channel_id=1, source_target_pairs={{0,1},{1,0},{2,3},{3,2},{4,5},{5,4},{6,7},{7,6},{8,9},{9,8},{10,11... | collective-permute-start | bytes 1990664 | tf_op jit(solution)/shard_map/ppermute | solution.py:305
  76.8 0.1 div.22
  76.9 0.6 copy.12
  77.5 1.7 %collective-permute-done.24 = f32[8,128]{1,0:T(8,128)S(1)} collective-permute-done((f32[8,128]{1,0:T(8,128)S(1)}, f32[8,128]{1,0:T(8,128)S(1)}, u32[]{:S(2)}, u32[]{:S(2)}) %collective-permute-start.24) | collective-permute-done | bytes 4128 | tf_op jit(solution)/shard_map/ppermute | solution.py:47
  79.3 15.2 %attend.1 = (f32[32,128]{1,0:T(8,128)S(1)}, f32[2048,128]{1,0:T(8,128)S(1)}, f32[2048,128]{1,0:T(8,128)S(1)}, f32[2048,128]{1,0:T(8,128)S(1)}) custom-call(s32[8]{0:T(128)S(1)} %stack.62.refs_0_, bf16[128,1024]{1,0:T(8,128)(2,1)S(1)} %collective-permute-done.refs_1_, bf16[128,1024]{1,0:T(8,128)(2,1)S(1)} %collective-permute-done.1.refs_2_, ...), custom_call_target="tpu_custom_call" | custom-call | flops 2684354560 | bytes 4194304 | tf_op jit(solution)/shard_map/attend/pallas_call | solution.py:228
  94.5 12.8 %attend_last.1 = (bf16[128,1024]{1,0:T(8,128)(2,1)S(1)}, bf16[128,1024]{1,0:T(8,128)(2,1)S(1)}) custom-call(s32[8]{0:T(128)S(1)} %stack.56.refs_0_, bf16[128,1024]{1,0:T(8,128)(2,1)S(1)} %collective-permute-done.refs_1_, bf16[128,1024]{1,0:T(8,128)(2,1)S(1)} %collective-permute-done.1.refs_2_, ...), custom_call_target="tpu_custom_call" | custom-call | flops 2415919104 | bytes 4194304 | tf_op jit(solution)/shard_map/attend_last/pallas_call | solution.py:228
  107.3 5.7 %collective-permute-start.15 = (bf16[128,1024]{1,0:T(8,128)(2,1)S(1)}, bf16[128,1024]{1,0:T(8,128)(2,1)S(1)}, u32[]{:S(2)}, u32[]{:S(2)}) collective-permute-start(bf16[128,1024]{1,0:T(8,128)(2,1)S(1)} %get-tuple-element.16), channel_id=1, source_target_pairs={{0,0},{8,1},{4,4},{12,5},{1,8},{9,9},{5,12},{13,13},{2,2},{10,3},{... | collective-permute-start | bytes 786440 | tf_op jit(solution)/shard_map/ppermute | solution.py:312
  113.1 0.1 collective-permute-start.16
  113.3 0.6 fusion.1
  113.9 4.6 %collective-permute-done.15 = bf16[128,1024]{1,0:T(8,128)(2,1)S(1)} collective-permute-done((bf16[128,1024]{1,0:T(8,128)(2,1)S(1)}, bf16[128,1024]{1,0:T(8,128)(2,1)S(1)}, u32[]{:S(2)}, u32[]{:S(2)}) %collective-permute-start.15) | collective-permute-done | bytes 262176 | tf_op jit(solution)/shard_map/ppermute | solution.py:312
  118.5 2.7 %collective-permute-done.16 = bf16[128,1024]{1,0:T(8,128)(2,1)S(1)} collective-permute-done((bf16[128,1024]{1,0:T(8,128)(2,1)S(1)}, bf16[128,1024]{1,0:T(8,128)(2,1)S(1)}, u32[]{:S(2)}, u32[]{:S(2)}) %collective-permute-start.16) | collective-permute-done | bytes 262176 | tf_op jit(solution)/shard_map/ppermute | solution.py:312
  121.2 0.9 maximum_select_fusion
  (49 shorter events, 0.5 us)
Async XLA Ops:
  0.6 0.7 copy-start.2
  4.0 5.4 %copy-start.1 = (bf16[2,2,128,32]{2,3,1,0:T(8,128)(2,1)S(1)}, bf16[2,2,128,32]{2,3,1,0:T(8,128)(2,1)}, u32[]{:S(2)}) copy-start(bf16[2,2,128,32]{2,3,1,0:T(8,128)(2,1)} %param.9) | copy-start | bytes 98308
  4.1 21.1 %collective-permute-start.2 = (bf16[144,256]{1,0:T(8,128)(2,1)S(1)}, bf16[144,256]{1,0:T(8,128)(2,1)S(1)}, u32[]{:S(2)}, u32[]{:S(2)}) collective-permute-start(bf16[144,256]{1,0:T(8,128)(2,1)S(1)} %get-tuple-element.33), channel_id=1, source_target_pairs={{0,0},{1,8},{4,4},{5,12},{8,1},{9,9},{12,5},{13,13},{2,2},{3,10},{... | collective-permute-start | bytes 221192 | tf_op jit(solution)/shard_map/ppermute | solution.py:267
  10.3 25.5 %copy-start = (bf16[128,2048]{1,0:T(8,128)(2,1)S(1)}, bf16[128,2048]{1,0:T(8,128)(2,1)}, u32[]{:S(2)}) copy-start(bf16[128,2048]{1,0:T(8,128)(2,1)} %param.5) | copy-start | bytes 1572868
  12.4 2.8 %collective-permute-start.17 = (f32[40,128]{1,0:T(8,128)}, f32[40,128]{1,0:T(8,128)S(1)}, u32[]{:S(2)}, u32[]{:S(2)}) collective-permute-start(f32[40,128]{1,0:T(8,128)} %get-tuple-element.19), channel_id=1, source_target_pairs={{0,4},{4,0},{8,12},{12,8},{1,5},{5,1},{9,13},{13,9},{2,6},{6,2},{1... | collective-permute-start | bytes 61448 | tf_op jit(solution)/shard_map/ppermute | solution.py:47
  16.0 4.1 %collective-permute-start.18 = (f32[40,128]{1,0:T(8,128)S(1)}, f32[40,128]{1,0:T(8,128)S(1)}, u32[]{:S(2)}, u32[]{:S(2)}) collective-permute-start(f32[40,128]{1,0:T(8,128)S(1)} %add.103), channel_id=1, source_target_pairs={{0,8},{4,12},{8,0},{12,4},{1,9},{5,13},{9,1},{13,5},{2,10},{6,14},... | collective-permute-start | bytes 61448 | tf_op jit(solution)/shard_map/ppermute | solution.py:47
  20.2 3.8 %collective-permute-start.19 = (f32[40,128]{1,0:T(8,128)S(1)}, f32[40,128]{1,0:T(8,128)S(1)}, u32[]{:S(2)}, u32[]{:S(2)}) collective-permute-start(f32[40,128]{1,0:T(8,128)S(1)} %add.104), channel_id=1, source_target_pairs={{0,16},{16,0},{32,48},{48,32},{64,80},{80,64},{96,112},{112,96},{1... | collective-permute-start | bytes 61448 | tf_op jit(solution)/shard_map/ppermute | solution.py:47
  20.9 7.2 %collective-permute-start.3 = (bf16[144,256]{1,0:T(8,128)(2,1)S(1)}, bf16[144,256]{1,0:T(8,128)(2,1)S(1)}, u32[]{:S(2)}, u32[]{:S(2)}) collective-permute-start(bf16[144,256]{1,0:T(8,128)(2,1)S(1)} %get-tuple-element.32), channel_id=1, source_target_pairs={{0,4},{1,12},{4,0},{5,8},{8,5},{9,13},{12,1},{13,9},{2,6},{3,14},{... | collective-permute-start | bytes 221192 | tf_op jit(solution)/shard_map/ppermute | solution.py:267
  24.0 3.8 %collective-permute-start.20 = (f32[40,128]{1,0:T(8,128)S(1)}, f32[40,128]{1,0:T(8,128)S(1)}, u32[]{:S(2)}, u32[]{:S(2)}) collective-permute-start(f32[40,128]{1,0:T(8,128)S(1)} %add.105), channel_id=1, source_target_pairs={{0,32},{16,48},{32,0},{48,16},{64,96},{80,112},{96,64},{112,80},{1... | collective-permute-start | bytes 61448 | tf_op jit(solution)/shard_map/ppermute | solution.py:47
  27.8 6.8 %collective-permute-start.21 = (f32[40,128]{1,0:T(8,128)S(1)}, f32[40,128]{1,0:T(8,128)S(1)}, u32[]{:S(2)}, u32[]{:S(2)}) collective-permute-start(f32[40,128]{1,0:T(8,128)S(1)} %add.106), channel_id=1, source_target_pairs={{0,64},{16,80},{32,96},{48,112},{64,0},{80,16},{96,32},{112,48},{1... | collective-permute-start | bytes 61448 | tf_op jit(solution)/shard_map/ppermute | solution.py:47
  28.1 16.2 %collective-permute-start.4 = (bf16[288,256]{1,0:T(8,128)(2,1)S(1)}, bf16[288,256]{1,0:T(8,128)(2,1)S(1)}, u32[]{:S(2)}, u32[]{:S(2)}) collective-permute-start(bf16[288,256]{1,0:T(8,128)(2,1)S(1)} %get-tuple-element.25), channel_id=1, source_target_pairs={{0,16},{16,32},{32,48},{48,64},{64,80},{80,96},{96,112},{112,128},... | collective-permute-start | bytes 442376 | tf_op jit(solution)/shard_map/ppermute | solution.py:42
  32.7 11.9 %collective-permute-start.7 = (bf16[288,256]{1,0:T(8,128)(2,1)S(1)}, bf16[288,256]{1,0:T(8,128)(2,1)S(1)}, u32[]{:S(2)}, u32[]{:S(2)}) collective-permute-start(bf16[288,256]{1,0:T(8,128)(2,1)S(1)} %get-tuple-element.25), channel_id=1, source_target_pairs={{0,128},{16,144},{32,160},{48,176},{64,192},{80,208},{96,224},{112... | collective-permute-start | bytes 442376 | tf_op jit(solution)/shard_map/ppermute | solution.py:42
  34.6 9.6 %collective-permute-start.22 = (f32[40,128]{1,0:T(8,128)S(1)}, f32[40,128]{1,0:T(8,128)S(1)}, u32[]{:S(2)}, u32[]{:S(2)}) collective-permute-start(f32[40,128]{1,0:T(8,128)S(1)} %add.107), channel_id=1, source_target_pairs={{0,128},{128,0},{1,129},{129,1},{2,130},{130,2},{3,131},{131,3},{4... | collective-permute-start | bytes 61448 | tf_op jit(solution)/shard_map/ppermute | solution.py:47
  36.6 42.6 %collective-permute-start = (bf16[128,1024]{1,0:T(8,128)(2,1)}, bf16[128,1024]{1,0:T(8,128)(2,1)S(1)}, u32[]{:S(2)}, u32[]{:S(2)}) collective-permute-start(bf16[128,1024]{1,0:T(8,128)(2,1)} %get-tuple-element.23), channel_id=1, source_target_pairs={{0,0},{1,8},{4,4},{5,12},{8,1},{9,9},{12,5},{13,13},{2,2},{3,10},{... | collective-permute-start | bytes 786440 | tf_op jit(solution)/shard_map/ppermute | solution.py:269
  43.0 36.3 %collective-permute-start.1 = (bf16[128,1024]{1,0:T(8,128)(2,1)}, bf16[128,1024]{1,0:T(8,128)(2,1)S(1)}, u32[]{:S(2)}, u32[]{:S(2)}) collective-permute-start(bf16[128,1024]{1,0:T(8,128)(2,1)} %get-tuple-element.22), channel_id=1, source_target_pairs={{0,4},{1,12},{4,0},{5,8},{8,5},{9,13},{12,1},{13,9},{2,6},{3,14},{... | collective-permute-start | bytes 786440 | tf_op jit(solution)/shard_map/ppermute | solution.py:269
  44.2 32.6 %collective-permute-start.23 = (f32[8,128]{1,0:T(8,128)S(1)}, f32[8,128]{1,0:T(8,128)S(1)}, u32[]{:S(2)}, u32[]{:S(2)}) collective-permute-start(f32[8,128]{1,0:T(8,128)S(1)} %slice.23), channel_id=1, source_target_pairs={{0,1},{1,0},{2,3},{3,2},{4,5},{5,4},{6,7},{7,6},{8,9},{9,8},{10,11... | collective-permute-start | bytes 12296 | tf_op jit(solution)/shard_map/ppermute | solution.py:47
  44.3 5.1 %collective-permute-start.5 = (bf16[288,256]{1,0:T(8,128)(2,1)S(1)}, bf16[288,256]{1,0:T(8,128)(2,1)S(1)}, u32[]{:S(2)}, u32[]{:S(2)}) collective-permute-start(bf16[288,256]{1,0:T(8,128)(2,1)S(1)} %collective-permute-done.4), channel_id=1, source_target_pairs={{0,16},{16,32},{32,48},{48,64},{64,80},{80,96},{96,112},{112,128},... | collective-permute-start | bytes 442376 | tf_op jit(solution)/shard_map/ppermute | solution.py:42
  44.7 8.8 %collective-permute-start.8 = (bf16[288,256]{1,0:T(8,128)(2,1)S(1)}, bf16[288,256]{1,0:T(8,128)(2,1)S(1)}, u32[]{:S(2)}, u32[]{:S(2)}) collective-permute-start(bf16[288,256]{1,0:T(8,128)(2,1)S(1)} %collective-permute-done.7), channel_id=1, source_target_pairs={{0,240},{16,0},{32,16},{48,32},{64,48},{80,64},{96,80},{112,96},{1... | collective-permute-start | bytes 442376 | tf_op jit(solution)/shard_map/ppermute | solution.py:42
  49.4 6.1 %collective-permute-start.6 = (bf16[288,256]{1,0:T(8,128)(2,1)S(1)}, bf16[288,256]{1,0:T(8,128)(2,1)S(1)}, u32[]{:S(2)}, u32[]{:S(2)}) collective-permute-start(bf16[288,256]{1,0:T(8,128)(2,1)S(1)} %collective-permute-done.5), channel_id=1, source_target_pairs={{0,16},{16,32},{32,48},{48,64},{64,80},{80,96},{96,112},{112,128},... | collective-permute-start | bytes 442376 | tf_op jit(solution)/shard_map/ppermute | solution.py:42
  53.4 7.7 %collective-permute-start.9 = (bf16[288,256]{1,0:T(8,128)(2,1)S(1)}, bf16[288,256]{1,0:T(8,128)(2,1)S(1)}, u32[]{:S(2)}, u32[]{:S(2)}) collective-permute-start(bf16[288,256]{1,0:T(8,128)(2,1)S(1)} %collective-permute-done.8), channel_id=1, source_target_pairs={{0,240},{16,0},{32,16},{48,32},{64,48},{80,64},{96,80},{112,96},{1... | collective-permute-start | bytes 442376 | tf_op jit(solution)/shard_map/ppermute | solution.py:42
  55.5 7.6 %collective-permute-start.10 = (bf16[288,256]{1,0:T(8,128)(2,1)S(1)}, bf16[288,256]{1,0:T(8,128)(2,1)S(1)}, u32[]{:S(2)}, u32[]{:S(2)}) collective-permute-start(bf16[288,256]{1,0:T(8,128)(2,1)S(1)} %collective-permute-done.6), channel_id=1, source_target_pairs={{0,16},{16,32},{32,48},{48,64},{64,80},{80,96},{96,112},{112,128},... | collective-permute-start | bytes 442376 | tf_op jit(solution)/shard_map/ppermute | solution.py:42
  61.1 7.6 %collective-permute-start.11 = (bf16[288,256]{1,0:T(8,128)(2,1)S(1)}, bf16[288,256]{1,0:T(8,128)(2,1)S(1)}, u32[]{:S(2)}, u32[]{:S(2)}) collective-permute-start(bf16[288,256]{1,0:T(8,128)(2,1)S(1)} %collective-permute-done.9), channel_id=1, source_target_pairs={{0,240},{16,0},{32,16},{48,32},{64,48},{80,64},{96,80},{112,96},{1... | collective-permute-start | bytes 442376 | tf_op jit(solution)/shard_map/ppermute | solution.py:42
  63.1 16.2 %collective-permute-start.14 = (bf16[1440,256]{1,0:T(8,128)(2,1)S(1)}, bf16[1440,256]{1,0:T(8,128)(2,1)S(1)}, u32[]{:S(2)}, u32[]{:S(2)}) collective-permute-start(bf16[1440,256]{1,0:T(8,128)(2,1)S(1)} %constant_dynamic-update-slice_fusion.7.refs_3_), channel_id=1, source_target_pairs={{0,1},{1,0},{2,3},{3,2},{4,5},{5,4},{6,7},{7,6},{8,9},{9,8},{10,11... | collective-permute-start | bytes 2211848 | tf_op jit(solution)/shard_map/ppermute | solution.py:305
  68.7 5.0 %collective-permute-start.12 = (bf16[144,256]{1,0:T(8,128)(2,1)S(1)}, bf16[144,256]{1,0:T(8,128)(2,1)S(1)}, u32[]{:S(2)}, u32[]{:S(2)}) collective-permute-start(bf16[144,256]{1,0:T(8,128)(2,1)S(1)} %slice_select_fusion), channel_id=1, source_target_pairs={{0,16},{16,32},{32,48},{48,64},{64,80},{80,96},{96,112},{112,128},... | collective-permute-start | bytes 221192 | tf_op jit(solution)/shard_map/ppermute | solution.py:42
  73.8 20.7 %collective-permute-start.13 = (bf16[1296,256]{1,0:T(8,128)(2,1)S(1)}, bf16[1296,256]{1,0:T(8,128)(2,1)S(1)}, u32[]{:S(2)}, u32[]{:S(2)}) collective-permute-start(bf16[1296,256]{1,0:T(8,128)(2,1)S(1)} %constant_dynamic-update-slice_fusion.2.refs_3_), channel_id=1, source_target_pairs={{0,1},{1,0},{2,3},{3,2},{4,5},{5,4},{6,7},{7,6},{8,9},{9,8},{10,11... | collective-permute-start | bytes 1990664 | tf_op jit(solution)/shard_map/ppermute | solution.py:305
  76.8 2.5 %collective-permute-start.24 = (f32[8,128]{1,0:T(8,128)S(1)}, f32[8,128]{1,0:T(8,128)S(1)}, u32[]{:S(2)}, u32[]{:S(2)}) collective-permute-start(f32[8,128]{1,0:T(8,128)S(1)} %slice_add_fusion), channel_id=1, source_target_pairs={{0,2},{2,0},{1,3},{3,1},{4,6},{6,4},{5,7},{7,5},{8,10},{10,8},{9,1... | collective-permute-start | bytes 12296 | tf_op jit(solution)/shard_map/ppermute | solution.py:47
  107.3 11.1 %collective-permute-start.15 = (bf16[128,1024]{1,0:T(8,128)(2,1)S(1)}, bf16[128,1024]{1,0:T(8,128)(2,1)S(1)}, u32[]{:S(2)}, u32[]{:S(2)}) collective-permute-start(bf16[128,1024]{1,0:T(8,128)(2,1)S(1)} %get-tuple-element.16), channel_id=1, source_target_pairs={{0,0},{8,1},{4,4},{12,5},{1,8},{9,9},{5,12},{13,13},{2,2},{10,3},{... | collective-permute-start | bytes 786440 | tf_op jit(solution)/shard_map/ppermute | solution.py:312
  113.1 8.1 %collective-permute-start.16 = (bf16[128,1024]{1,0:T(8,128)(2,1)S(1)}, bf16[128,1024]{1,0:T(8,128)(2,1)S(1)}, u32[]{:S(2)}, u32[]{:S(2)}) collective-permute-start(bf16[128,1024]{1,0:T(8,128)(2,1)S(1)} %get-tuple-element.17), channel_id=1, source_target_pairs={{4,0},{12,1},{0,4},{8,5},{5,8},{13,9},{1,12},{9,13},{6,2},{14,3},{... | collective-permute-start | bytes 786440 | tf_op jit(solution)/shard_map/ppermute | solution.py:312
